TPU v7x, 32 devices: a whole 2x2x4 slice. The times are simulated.
32 devices in a mesh: dp: 4 (over y, x), vocab: 8 (over z, core).
Axes of the slice: x: 2, y: 2, z: 4, core: 2. Of those that a mesh axis runs over, the one named last changes fastest.
Arguments:
- hidden: bfloat16 [1024, 8192], P('dp'), may hold values from -14 to 14
- weight: bfloat16 [8192, 8192], P('dp', 'vocab'), may hold values from -1 to 1, as said below
- targets: int32 [1024], P('dp'), may hold values from 0 to 8191
- cotangent: float32 [1024], P('dp'), may hold values from 1 to 8
Outputs:
- loss: float32 [1024], P('dp')
- grad_hidden: bfloat16 [1024, 8192], P('vocab', 'dp')
- grad_weight: bfloat16 [8192, 8192], P('dp', 'vocab')
Inputs may be any that keep to these rules, and one draw needn't show every extreme that they name: `weight`: entries drawn with standard deviation 4 / sqrt(8192).
All inputs are finite; a program needn't handle non-finite values.
Results may differ from a plain program's by a relative error of at most 0.0047.
Values may be sent and summed in bfloat16 or wider, within the bound.
A program may use at most 128 MiB of HBM per device.

v0:
```python
import jax
import jax.numpy as jnp
from jax import lax
from jax.sharding import PartitionSpec as P


def shards(hidden, weight, targets, cotangent):
    vocab_width = weight.shape[1]
    spread = lax.all_to_all(hidden, "dp", split_axis=1, concat_axis=0, tiled=True)
    vocab_first = lax.axis_index("vocab") * vocab_width
    columns = vocab_first + lax.iota(jnp.int32, vocab_width)
    onehot = (targets[:, None] == columns[None, :]).astype(jnp.float32)
    row_block = spread
    logits = lax.psum_scatter(
        jnp.dot(row_block, weight, preferred_element_type=jnp.float32),
        "dp",
        scatter_dimension=0,
        tiled=True,
    )
    local_max = jnp.max(logits, axis=1)
    local_pick = jnp.sum(logits * onehot, axis=1)
    row_max = lax.pmax(local_max, "vocab")
    shifted = jnp.exp(logits - row_max[:, None])
    sum_exp, picked = lax.psum((jnp.sum(shifted, axis=1), local_pick), "vocab")
    loss = row_max + jnp.log(sum_exp) - picked
    grad_logits = (cotangent[:, None] * (shifted / sum_exp[:, None] - onehot)).astype(jnp.bfloat16)
    all_grads = lax.all_gather(grad_logits, "dp", axis=0, tiled=True)
    grad_weight = lax.dot_general(
        spread, all_grads, (((0,), (0,)), ((), ())), preferred_element_type=jnp.float32
    ).astype(jnp.bfloat16)
    row_block = all_grads
    grad_hidden = lax.psum_scatter(
        lax.dot_general(
            row_block, weight, (((1,), (1,)), ((), ())), preferred_element_type=jnp.float32
        ),
        "vocab",
        scatter_dimension=0,
        tiled=True,
    ).astype(jnp.bfloat16)
    return (loss, grad_hidden, grad_weight)


def solution(mesh):
    in_specs = (P("dp", None), P("dp", "vocab"), P("dp"), P("dp"))
    out_specs = (P("dp"), P("vocab", "dp"), P("dp", "vocab"))
    return jax.shard_map(shards, mesh=mesh, in_specs=in_specs, out_specs=out_specs, check_vma=False)
```

profile of v0, /device:TPU:8, one launch (start us, length us, event | category | flops | bytes accessed | tf_op | source)
XLA Modules:
  0.0 309.7 jit_solution(2251081179240819122)
XLA Ops:
  7.2 0.0 reduce-scatter.3.cloned.1.call-start
  7.2 6.4 %copy.9 = bf16[256,8192]{0,1:T(8,128)(2,1)} copy(bf16[256,8192]{1,0:T(8,128)(2,1)} %param.4) | data formatting | bytes 8388608 | tf_op args[0]
  13.6 53.8 %all_to_all.19 = bf16[256,4,2048]{0,2,1:T(8,128)(2,1)} all-to-all(bf16[256,4,2048]{0,2,1:T(8,128)(2,1)} %bitcast.12), channel_id=1, replica_groups=mesh['dp'=4,'vocab'=8] {'dp'}, dimensions={1} | all-to-all | bytes 8388608 | tf_op jit(solution)/shard_map/all_to_all | solution.py:9
  67.4 6.2 %copy.10 = bf16[4,256,2048]{2,1,0:T(8,128)(2,1)} copy(bf16[4,256,2048]{1,2,0:T(8,128)(2,1)} %bitcast.11) | data formatting | bytes 8388608 | tf_op jit(solution)/shard_map/all_to_all | solution.py:9
  73.6 9.9 %fusion.5 = f32[1024,1024]{1,0:T(8,128)} fusion(bf16[1024,2048]{1,0:T(8,128)(2,1)} %bitcast.13, bf16[2048,1024]{1,0:T(8,128)(2,1)} %param.5), kind=kOutput, calls=%fused_computation.11 | convolution fusion | flops 4294967296 | bytes 12582912 | tf_op jit(solution)/shard_map/dot_general | solution.py:15
  83.5 0.0 copy-start
  83.5 0.0 copy-start.1
  83.5 0.0 reduce-scatter.3.cloned.1.call-update
  83.5 0.0 all-gather.2.cloned.1.call-start
  83.5 52.3 %reduce-scatter.3.cloned.1.call-done = f32[256,1024]{1,0:T(8,128)} async-done(((f32[1024,1024]{1,0:T(8,128)}), f32[256,1024]{1,0:T(8,128)}) %reduce-scatter.3.cloned.1.call-update) | async-done | bytes 1048592 | tf_op jit(solution)/shard_map/reduce_scatter | solution.py:14
  135.9 1.4 reduce_max.9
  137.2 12.7 %pmax.7 = f32[256]{0:T(256)S(1)} all-reduce(f32[256]{0:T(256)S(1)} %reduce_max.9), channel_id=1, replica_groups=mesh['dp'=4,'vocab'=8] {'vocab'}, use_global_device_ids=true, to_apply=%region_2.0 | all-reduce | flops 256 | bytes 2048 | tf_op jit(solution)/shard_map/pmax | solution.py:22
  149.9 0.0 copy-done
  149.9 1.6 fusion.4
  151.5 13.6 %all-reduce = (f32[256]{0:T(256)S(1)}, f32[256]{0:T(256)S(1)}) all-reduce(f32[256]{0:T(256)S(1)} %get-tuple-element.13, f32[256]{0:T(256)S(1)} %get-tuple-element.12), channel_id=1, replica_groups=mesh['dp'=4,'vocab'=8] {'vocab'}, use_global_device_ids=true, to_apply=%region_6.0 | all-reduce | flops 512 | bytes 4096 | tf_op jit(solution)/shard_map/psum | solution.py:24
  165.1 0.0 copy-done.1
  165.1 2.4 fusion.3
  167.5 0.0 all-gather.2.cloned.1.call-update
  167.5 0.0 reduce-scatter.5.cloned.1.call-start
  167.5 36.0 %all-gather.2.cloned.1.call-done = bf16[1024,1024]{1,0:T(8,128)(2,1)} async-done(((bf16[256,1024]{1,0:T(8,128)(2,1)}), bf16[1024,1024]{1,0:T(8,128)(2,1)}) %all-gather.2.cloned.1.call-update) | async-done | bytes 2097168 | tf_op jit(solution)/shard_map/all_gather | solution.py:27
  203.6 10.6 %fusion.6 = f32[1024,2048]{1,0:T(8,128)} fusion(bf16[1024,1024]{1,0:T(8,128)(2,1)} %all-gather.2.cloned.1.call-done, bf16[2048,1024]{1,0:T(8,128)(2,1)} %param.5), kind=kOutput, calls=%fused_computation.12 | convolution fusion | flops 4294967296 | bytes 14680064 | tf_op jit(solution)/shard_map/dot_general | solution.py:33
  214.2 0.0 copy-start.2
  214.2 0.0 reduce-scatter.5.cloned.1.call-update
  214.2 0.6 add_subtract_fusion
  214.8 1.0 copy-done.2
  215.7 8.3 %convert_bitcast_fusion = bf16[2048,1024]{0,1:T(8,128)(2,1)} fusion(bf16[1024,1024]{1,0:T(8,128)(2,1)S(1)} %copy-done.2, bf16[1024,2048]{1,0:T(8,128)(2,1)} %bitcast.14), kind=kOutput, calls=%fused_computation | convolution fusion | flops 4297064448 | bytes 10485760 | tf_op jit(solution)/shard_map/dot_general | solution.py:28
  224.0 6.4 %copy.11 = bf16[2048,1024]{1,0:T(8,128)(2,1)} copy(bf16[2048,1024]{0,1:T(8,128)(2,1)} %convert_bitcast_fusion) | data formatting | bytes 8388608
  230.4 70.6 %reduce-scatter.5.cloned.1.call-done = f32[128,2048]{1,0:T(8,128)} async-done(((f32[1024,2048]{1,0:T(8,128)}), f32[128,2048]{1,0:T(8,128)}) %reduce-scatter.5.cloned.1.call-update) | async-done | bytes 1048592 | tf_op jit(solution)/shard_map/reduce_scatter | solution.py:32
  301.1 2.1 convert_element_type.17
  (1 shorter events, 0.0 us)
Async XLA Ops:
  7.2 128.7 %reduce-scatter.3.cloned.1.call-start = ((), (), s32[]{:S(2)}) async-start(), calls=%async_computation.3 | async-start | bytes 5242880 | tf_op jit(solution)/shard_map/reduce_scatter | solution.py:14
  83.5 66.4 %copy-start = (s32[256]{0:T(256)S(1)}, s32[256]{0:T(256)}, u32[]{:S(2)}) copy-start(s32[256]{0:T(256)} %param.6) | copy-start | bytes 3076
  83.5 81.6 %copy-start.1 = (f32[256]{0:T(256)S(1)}, f32[256]{0:T(256)}, u32[]{:S(2)}) copy-start(f32[256]{0:T(256)} %param.7) | copy-start | bytes 3076
  83.5 120.1 %all-gather.2.cloned.1.call-start = ((), (), s32[]{:S(2)}) async-start(), calls=%async_computation.4 | async-start | bytes 2621440 | tf_op jit(solution)/shard_map/all_gather | solution.py:27
  167.5 133.6 %reduce-scatter.5.cloned.1.call-start = ((), (), s32[]{:S(2)}) async-start(), calls=%async_computation.5 | async-start | bytes 9437184 | tf_op jit(solution)/shard_map/reduce_scatter | solution.py:32
  214.2 1.6 copy-start.2
Sparse Core Ops, SparseCore 0:
  83.6 52.2 reduce-scatter.2
  167.6 35.9 all-gather.1
  214.3 86.7 reduce-scatter.4
where the time goes:
time: 315 us; the launch traced here: 310 us
  waiting for transfers between devices  159 us (50%)
  blocking collectives  80.1 us (25%)
  matrix products  28.7 us (9%)
  local copies, waits for them, and re-layouts  20 us (6%)
  between operations  13.8 us (4%)
  other arithmetic  8 us (3%)
    reduce_scatter x1, waiting for transfers between devices, shards(): lax.psum_scatter(lax.dot_general(row_block, weight, (((1,), (1,)), ((), (...  70.6 us
    all_to_all x1, blocking collectives, shards(): lax.all_to_all(hidden, 'dp', split_axis=1, concat_axis=0, tiled=True)  53.8 us
    reduce_scatter x1, waiting for transfers between devices, shards(): lax.psum_scatter(jnp.dot(row_block, weight, preferred_element_type=jnp.fl...  52.3 us
    all_gather x1, waiting for transfers between devices, shards(): all_grads = lax.all_gather(grad_logits, 'dp', axis=0, tiled=True)  36 us
    unnamed x8, local copies, waits for them, and re-layouts  13.8 us
    psum x1, blocking collectives, shards(): sum_exp, picked = lax.psum((jnp.sum(shifted, axis=1), local_pick), 'vocab')  13.6 us
    pmax x1, blocking collectives, shards(): row_max = lax.pmax(local_max, 'vocab')  12.7 us
    dot_general x1, matrix products, shards(): lax.dot_general(row_block, weight, (((1,), (1,)), ((), ())), preferred_el...  10.6 us
  transfers between devices with their start and end apart: 3, of which 3 were waited for; matrix products, arithmetic and copies ran while one was open for 5% of the time, Pallas kernels for 0%

commit v1 on v0

v1 whole, which is shorter than its diff:
```python
import functools

import jax
import jax.numpy as jnp
from jax import lax
from jax.experimental import pallas as pl
from jax.experimental.pallas import tpu as pltpu
from jax.sharding import PartitionSpec as P

F32 = jnp.float32
BF16 = jnp.bfloat16
WIRE = jnp.int16
STEPS = 32000.0


def kernel(
    nd, nv, levels,
    h_ref, w_hbm, t_ref, c_ref,
    loss_ref, gh_ref, gw_ref,
    w, spread, logit, psend, precv, stats, grads, acc, sbuf, rbuf, gwbuf, tcol, ccol, col,
    part_f32, usend, urecv, ucol,
    w_sem, own_sem, gw_sem,
    hs_send, hs_recv, hf_send, hf_recv, p_send, p_recv, u_send, u_recv,
    st_send, st_recv, g_send, g_recv, r_send, r_recv,
):
    d, v = lax.axis_index("dp"), lax.axis_index("vocab")
    core = lax.rem(v, 2)
    mate = v + 1 - 2 * core
    depth, width = w.shape
    tokens = spread.shape[0]
    rows = tokens // nd
    half = rows // 2
    share = tokens // nv
    per = rows // share

    load_w = pltpu.make_async_copy(w_hbm, w, w_sem)
    load_w.start()
    own_rows = pl.ds(pl.multiple_of(d * rows, rows), rows)
    load_own = pltpu.make_async_copy(
        h_ref.at[:, pl.ds(pl.multiple_of(d * depth, depth), depth)], spread.at[own_rows], own_sem
    )
    load_own.start()

    barrier = pltpu.get_barrier_semaphore()
    for k in range(1, nd):
        pl.semaphore_signal(barrier, inc=1, device_id={"dp": lax.rem(d + k, nd)})
    for k in range(1, nv):
        pl.semaphore_signal(barrier, inc=1, device_id={"vocab": lax.rem(v + k, nv)})
    pl.semaphore_wait(barrier, nd + nv - 2)

    def remote(src, dst, send, recv, where):
        return pltpu.make_async_remote_copy(
            src_ref=src, dst_ref=dst, send_sem=send, recv_sem=recv, device_id=where
        )

    hidden_sends = []
    for k in range(1, nd):
        to = lax.rem(d + k, nd)
        copy = remote(
            h_ref.at[pl.ds(pl.multiple_of(core * half, half), half), pl.ds(pl.multiple_of(to * depth, depth), depth)],
            spread.at[pl.ds(pl.multiple_of(d * rows + core * half, half), half)],
            hs_send.at[k - 1], hs_recv.at[k - 1], {"dp": to},
        )
        copy.start()
        hidden_sends.append(copy)

    tcol[...] = jnp.broadcast_to(t_ref[...], (128, rows)).T
    ccol[...] = jnp.broadcast_to(c_ref[...], (128, rows)).T

    tile = min(256, width)
    code_rows = min(32, half)

    def project(first, count, store):
        def step(n, _):
            cols = pl.ds(pl.multiple_of(n * tile, tile), tile)
            store(cols, jnp.dot(
                spread[pl.ds(pl.multiple_of(first, count), count), :], w[:, cols],
                preferred_element_type=F32,
            ))
            return 0

        lax.fori_loop(0, width // tile, step, 0)

    load_w.wait()
    load_own.wait()

    def store_own(cols, value):
        logit[:, cols] = value

    project(d * rows, rows, store_own)

    forwards, partial_sends = [], []
    for k in range(1, nd):
        s = lax.rem(d + nd - k, nd)
        for turn in range(2):
            part = core if turn == 0 else 1 - core
            block = spread.at[pl.ds(pl.multiple_of(s * rows + part * half, half), half)]
            if turn == 0:
                remote(block, block, hs_send.at[k - 1], hs_recv.at[k - 1], {"dp": s}).wait_recv()
                copy = remote(block, block, hf_send.at[k - 1], hf_recv.at[k - 1], {"vocab": mate})
                copy.start()
                forwards.append(copy)
            else:
                remote(block, block, hf_send.at[k - 1], hf_recv.at[k - 1], {"vocab": mate}).wait_recv()
            there = pl.ds(pl.multiple_of(part * half, half), half)

            def store_part(cols, value):
                part_f32[:, cols] = value

            project(s * rows + part * half, half, store_part)

            def encode(i, _, k=k, part=part):
                at = pl.ds(pl.multiple_of(i * code_rows, code_rows), code_rows)
                x = part_f32[at, :]
                unit = jnp.maximum(jnp.max(jnp.abs(x), axis=1, keepdims=True), 1e-30) / STEPS
                there = pl.ds(pl.multiple_of(part * half + i * code_rows, code_rows), code_rows)
                psend[k - 1, there, :] = jnp.round(x / unit).astype(jnp.int32).astype(WIRE)
                col[at, :] = jnp.broadcast_to(unit, (code_rows, 128))
                return 0

            lax.fori_loop(0, half // code_rows, encode, 0)
            usend[k - 1, turn] = col[:half, :].T[:8, :]
            for copy in (
                remote(
                    psend.at[k - 1, there], precv.at[k - 1, there],
                    p_send.at[k - 1, turn], p_recv.at[k - 1, turn], {"dp": s},
                ),
                remote(
                    usend.at[k - 1, turn], urecv.at[k - 1, turn],
                    u_send.at[k - 1, turn], u_recv.at[k - 1, turn], {"dp": s},
                ),
            ):
                copy.start()
                partial_sends.append(copy)
    for copy in partial_sends:
        copy.wait_recv()
    for k in range(1, nd):
        for turn in range(2):
            part = core if turn == 0 else 1 - core
            there = pl.ds(pl.multiple_of(part * half, half), half)
            ucol[k - 1, there, :] = jnp.broadcast_to(urecv[k - 1, turn][0:1, :], (128, half)).T

    step_rows = min(32, rows)
    column = lax.broadcasted_iota(jnp.int32, (step_rows, width), 1) + v * width
    lane = lax.broadcasted_iota(jnp.int32, (step_rows, 128), 1)

    def measure(i, _):
        at = pl.ds(pl.multiple_of(i * step_rows, step_rows), step_rows)
        x = logit[at, :]
        for k in range(1, nd):
            x = x + precv[k - 1, at, :].astype(jnp.int32).astype(F32) * ucol[k - 1, at, :1]
        top = jnp.max(x, axis=1, keepdims=True)
        e = jnp.exp(x - top)
        total = jnp.sum(e, axis=1, keepdims=True)
        pick = jnp.sum(jnp.where(column == tcol[at, :1], x, 0.0), axis=1, keepdims=True)
        logit[at, :] = e
        col[at, :] = jnp.where(lane == 0, top, jnp.where(lane == 1, total, pick))
        return 0

    lax.fori_loop(0, rows // step_rows, measure, 0)
    stats[v] = col[...].T[:8, :]
    stat_sends = []
    for k in range(1, nv):
        copy = remote(
            stats.at[v], stats.at[v], st_send.at[k - 1], st_recv.at[k - 1],
            {"vocab": lax.rem(v + k, nv)},
        )
        copy.start()
        stat_sends.append(copy)
    own_top = stats[v][0:1, :]
    for copy in stat_sends:
        copy.wait_recv()
    top = stats[0][0:1, :]
    for u in range(1, nv):
        top = jnp.maximum(top, stats[u][0:1, :])
    total = jnp.zeros_like(top)
    pick = jnp.zeros_like(top)
    for u in range(nv):
        block = stats[u]
        total = total + block[1:2, :] * jnp.exp(block[0:1, :] - top)
        pick = pick + block[2:3, :]
    loss_ref[...] = top + jnp.log(total) - pick
    scale = c_ref[...] * jnp.exp(own_top - top) / total
    col[...] = jnp.broadcast_to(scale, (128, rows)).T

    def differentiate(i, _):
        at = pl.ds(pl.multiple_of(i * step_rows, step_rows), step_rows)
        onehot = jnp.where(column == tcol[at, :1], ccol[at, :1], 0.0)
        g = logit[at, :] * col[at, :1] - onehot
        grads[pl.ds(pl.multiple_of(d * rows + i * step_rows, step_rows), step_rows), :] = g.astype(BF16)
        return 0

    lax.fori_loop(0, rows // step_rows, differentiate, 0)
    grad_sends = []
    for k in range(1, nd):
        copy = remote(
            grads.at[own_rows], grads.at[own_rows], g_send.at[k - 1], g_recv.at[k - 1],
            {"dp": lax.rem(d + k, nd)},
        )
        copy.start()
        grad_sends.append(copy)

    depth_tile = min(256, depth)

    def pull(k):
        s = lax.rem(d + nd - k, nd)

        def step(n, _):
            at = pl.ds(pl.multiple_of(n * depth_tile, depth_tile), depth_tile)
            value = lax.dot_general(
                grads[pl.ds(pl.multiple_of(s * rows, rows), rows), :], w[at, :],
                (((1,), (1,)), ((), ())), preferred_element_type=F32,
            )
            for j in range(per):
                acc[k * per + j, :, at] = value[j * share:(j + 1) * share, :]
            return 0

        lax.fori_loop(0, depth // depth_tile, step, 0)

    def ahead(b):
        s = lax.rem(d + nd - b // per, nd)
        return s * per + b % per - v + nv

    def partner(level):
        bit = lax.rem(v // (1 << level), 2)
        return {"vocab": v + (1 - 2 * bit) * (1 << level)}

    chunk = min(16, share)

    def hop(b, level):
        return remote(sbuf.at[b], rbuf.at[level, b], r_send.at[b], r_recv.at[level, b], partner(level))

    def each_chunk(body):
        def step(i, _):
            body(pl.ds(pl.multiple_of(i * chunk, chunk), chunk))
            return 0

        lax.fori_loop(0, share // chunk, step, 0)

    def send(b, level):
        mine = lax.rem(ahead(b), 1 << level) == 0
        leaves = lax.rem(ahead(b), 2 << level) != 0

        @pl.when(jnp.logical_and(mine, leaves))
        def _():
            def body(at):
                sbuf[b, at, :] = acc[b, at, :].astype(BF16)

            each_chunk(body)
            hop(b, level).start()

    def receive(b, level):
        @pl.when(lax.rem(ahead(b), 2 << level) == 0)
        def _():
            hop(b, level).wait_recv()

            def body(at):
                acc[b, at, :] = acc[b, at, :] + rbuf[level, b, at, :].astype(F32)

            each_chunk(body)

        if level + 1 < levels:
            send(b, level + 1)

    for k in range(nd):
        if k:
            grad_sends[k - 1].wait_recv()
        pull(k)
        for j in range(per):
            send(k * per + j, 0)
        if k:
            for j in range(per):
                receive((k - 1) * per + j, 0)
    for j in range(per):
        receive((nd - 1) * per + j, 0)

    def weigh(n, _):
        at = pl.ds(pl.multiple_of(n * depth_tile, depth_tile), depth_tile)
        gwbuf[at, :] = lax.dot_general(
            spread[:, at], grads[...], (((0,), (0,)), ((), ())), preferred_element_type=F32
        ).astype(BF16)
        pltpu.make_async_copy(gwbuf.at[at], gw_ref.at[at], gw_sem.at[n]).start()
        return 0

    lax.fori_loop(0, depth // depth_tile, weigh, 0)

    for level in range(1, levels):
        for b in range(nv):
            receive(b, level)
    for b in range(nv):
        @pl.when(ahead(b) == nv)
        def _(b=b):
            def body(at):
                gh_ref[at, :] = acc[b, at, :].astype(BF16)

            each_chunk(body)

        @pl.when(ahead(b) != nv)
        def _(b=b):
            hop(b, 0).wait_send()

    for copy in hidden_sends + forwards + partial_sends + stat_sends + grad_sends:
        copy.wait_send()
    for n in range(depth // depth_tile):
        at = pl.ds(n * depth_tile, depth_tile)
        pltpu.make_async_copy(gwbuf.at[at], gw_ref.at[at], gw_sem.at[n]).wait()


def shards(nd, nv, hidden, weight, targets, cotangent):
    rows = hidden.shape[0]
    tokens = rows * nd
    depth, width = weight.shape
    share = tokens // nv
    levels = nv.bit_length() - 1
    dma = pltpu.SemaphoreType.DMA
    vmem = pl.BlockSpec(memory_space=pltpu.VMEM)
    anywhere = pl.BlockSpec(memory_space=pl.ANY)
    flops = 6 * tokens * depth * width
    loss, grad_hidden, grad_weight = pl.pallas_call(
        functools.partial(kernel, nd, nv, levels),
        out_shape=(
            jax.ShapeDtypeStruct((1, rows), F32),
            jax.ShapeDtypeStruct((share, depth), BF16),
            jax.ShapeDtypeStruct((depth, width), BF16),
        ),
        in_specs=[anywhere, anywhere, vmem, vmem],
        out_specs=(vmem, vmem, anywhere),
        scratch_shapes=[
            pltpu.VMEM((depth, width), BF16),
            pltpu.VMEM((tokens, depth), BF16),
            pltpu.VMEM((rows, width), F32),
            pltpu.VMEM((nd - 1, rows, width), WIRE),
            pltpu.VMEM((nd - 1, rows, width), WIRE),
            pltpu.VMEM((nv, 8, rows), F32),
            pltpu.VMEM((tokens, width), BF16),
            pltpu.VMEM((nv, share, depth), F32),
            pltpu.VMEM((nv, share, depth), BF16),
            pltpu.VMEM((levels, nv, share, depth), BF16),
            pltpu.VMEM((depth, width), BF16),
            pltpu.VMEM((rows, 128), jnp.int32),
            pltpu.VMEM((rows, 128), F32),
            pltpu.VMEM((rows, 128), F32),
            pltpu.VMEM((rows // 2, width), F32),
            pltpu.VMEM((nd - 1, 2, 8, rows // 2), F32),
            pltpu.VMEM((nd - 1, 2, 8, rows // 2), F32),
            pltpu.VMEM((nd - 1, rows, 128), F32),
            dma, dma, dma((depth // min(256, depth),)),
            dma((nd - 1,)), dma((nd - 1,)), dma((nd - 1,)), dma((nd - 1,)),
            dma((nd - 1, 2)), dma((nd - 1, 2)), dma((nd - 1, 2)), dma((nd - 1, 2)),
            dma((nv - 1,)), dma((nv - 1,)),
            dma((nd - 1,)), dma((nd - 1,)),
            dma((nv,)), dma((levels, nv)),
        ],
        compiler_params=pltpu.CompilerParams(
            collective_id=0, has_side_effects=True, vmem_limit_bytes=66_000_000
        ),
        cost_estimate=pl.CostEstimate(flops=flops, bytes_accessed=16 << 20, transcendentals=0),
        name="token_loss",
    )(hidden, weight, targets.reshape(1, rows), cotangent.reshape(1, rows))
    return loss.reshape(rows), grad_hidden, grad_weight


def solution(mesh):
    in_specs = (P("dp", None), P("dp", "vocab"), P("dp"), P("dp"))
    out_specs = (P("dp"), P("vocab", "dp"), P("dp", "vocab"))
    body = functools.partial(shards, mesh.shape["dp"], mesh.shape["vocab"])
    return jax.shard_map(body, mesh=mesh, in_specs=in_specs, out_specs=out_specs, check_vma=False)
```

time: 315 us -> 146 us (0.46); the launches traced: 310 us -> 146 us
  waiting for transfers between devices: 159 us -> 0 us
  Pallas kernels: 0 us -> 137 us
  blocking collectives: 80.1 us -> 0 us
  matrix products: 28.7 us -> 0 us
  between operations: 13.8 us -> 0.64 us
  local copies, waits for them, and re-layouts: 20 us -> 7.75 us
  other arithmetic: 8 us -> 0 us
    pallas_call x0 -> x1, Pallas kernels: none -> 137 us  [shards(): pl.pallas_call(functools.partial(kernel, nd, nv, levels), out_shape=(jax....]
    reduce_scatter x2 -> x0, waiting for transfers between devices: 123 us -> none  [the longest x1 70.6 us: shards(): lax.psum_scatter(lax.dot_general(row_block, weight, (((1,), (1,)), ((), (...]
    all_to_all x1 -> x0, blocking collectives: 53.8 us -> none  [shards(): lax.all_to_all(hidden, 'dp', split_axis=1, concat_axis=0, tiled=True)]
    all_gather x1 -> x0, waiting for transfers between devices: 36 us -> none  [shards(): all_grads = lax.all_gather(grad_logits, 'dp', axis=0, tiled=True)]
    dot_general x3 -> x0, matrix products: 28.7 us -> none  [the longest x1 10.6 us: shards(): lax.dot_general(row_block, weight, (((1,), (1,)), ((), ())), preferred_el...]
    psum x1 -> x0, blocking collectives: 13.6 us -> none  [shards(): sum_exp, picked = lax.psum((jnp.sum(shifted, axis=1), local_pick), 'vocab')]
    pmax x1 -> x0, blocking collectives: 12.7 us -> none  [shards(): row_max = lax.pmax(local_max, 'vocab')]
    all_to_all x1 -> x0, local copies, waits for them, and re-layouts: 6.19 us -> none  [shards(): lax.all_to_all(hidden, 'dp', split_axis=1, concat_axis=0, tiled=True)]
  transfers between devices with their start and end apart: 3 -> 0, of which waited for: 3 -> 0; matrix products, arithmetic and copies ran while one was open for 5% -> 0% of each run, Pallas kernels for 0% -> 0%
where the time goes in v1:
time: 146 us
  Pallas kernels  137 us (94%)
  local copies, waits for them, and re-layouts  7.75 us (5%)
    pallas_call x1, Pallas kernels, shards(): pl.pallas_call(functools.partial(kernel, nd, nv, levels), out_shape=(jax....  137 us
    unnamed x3, local copies, waits for them, and re-layouts  7.75 us

profile of v1, /device:TPU:8, one launch (start us, length us, event | category | flops | bytes accessed | tf_op | source)
XLA Modules:
  0.0 145.6 jit_solution(16316655102576782806)
XLA Ops:
  0.6 137.2 %token_loss.1 = (f32[1,256]{1,0:T(1,128)}, bf16[128,2048]{1,0:T(8,128)(2,1)}, bf16[2048,1024]{1,0:T(8,128)(2,1)}) custom-call(bf16[256,8192]{1,0:T(8,128)(2,1)} %h_ref.1, bf16[2048,1024]{1,0:T(8,128)(2,1)} %w_hbm.1, s32[1,256]{1,0:T(1,128)} %bitcast.4, f32[1,256]{1,0:T(1,128)} %bitcast.5), custom_call_target="tpu_custom_call" | custom-call | flops 12884901888 | bytes 16777216 | tf_op jit(solution)/shard_map/token_loss/pallas_call | solution.py:319
  137.9 1.2 copy.10
  139.1 1.9 %copy.11 = bf16[128,2048]{1,0:T(8,128)(2,1)} copy(bf16[128,2048]{1,0:T(8,128)(2,1)} %get-tuple-element.13) | data formatting | bytes 1048576
  141.0 4.6 %copy.12 = bf16[2048,1024]{1,0:T(8,128)(2,1)} copy(bf16[2048,1024]{1,0:T(8,128)(2,1)} %get-tuple-element.14) | data formatting | bytes 8388608

commit v2 on v1

--- a/solution.py
+++ b/solution.py
@@ -20,16 +20,25 @@
     w, spread, logit, psend, precv, stats, grads, acc, sbuf, rbuf, gwbuf, tcol, ccol, col,
     part_f32, usend, urecv, ucol,
     w_sem, own_sem, gw_sem,
-    hs_send, hs_recv, hf_send, hf_recv, p_send, p_recv, u_send, u_recv,
-    st_send, st_recv, g_send, g_recv, r_send, r_recv,
+    hs_send, hs_recv, hf_send, hf_recv, hx_send, hx_recv, p_send, p_recv, u_send, u_recv,
+    st_send, st_recv, g_send, g_recv, x_send, x_recv, r_send, r_recv,
 ):
     d, v = lax.axis_index("dp"), lax.axis_index("vocab")
     core = lax.rem(v, 2)
-    mate = v + 1 - 2 * core
+
+    def flip(i, mask):
+        for bit in range(mask.bit_length()):
+            if mask >> bit & 1:
+                i = i + (1 - 2 * lax.rem(i // (1 << bit), 2)) * (1 << bit)
+        return i
+
+    mate, across = flip(v, 1), flip(v, 2)
+    side = lax.rem(v // 2, 2)
     depth, width = w.shape
     tokens = spread.shape[0]
     rows = tokens // nd
     half = rows // 2
+    quarter = rows // 4
     share = tokens // nv
     per = rows // share
 
@@ -43,7 +52,7 @@
 
     barrier = pltpu.get_barrier_semaphore()
     for k in range(1, nd):
-        pl.semaphore_signal(barrier, inc=1, device_id={"dp": lax.rem(d + k, nd)})
+        pl.semaphore_signal(barrier, inc=1, device_id={"dp": flip(d, k)})
     for k in range(1, nv):
         pl.semaphore_signal(barrier, inc=1, device_id={"vocab": lax.rem(v + k, nv)})
     pl.semaphore_wait(barrier, nd + nv - 2)
@@ -53,13 +62,19 @@
             src_ref=src, dst_ref=dst, send_sem=send, recv_sem=recv, device_id=where
         )
 
+    def piece(s, q):
+        return spread.at[pl.ds(pl.multiple_of(s * rows + q * quarter, quarter), quarter)]
+
+    mine = 2 * side + core
     hidden_sends = []
     for k in range(1, nd):
-        to = lax.rem(d + k, nd)
+        to = flip(d, k)
         copy = remote(
-            h_ref.at[pl.ds(pl.multiple_of(core * half, half), half), pl.ds(pl.multiple_of(to * depth, depth), depth)],
-            spread.at[pl.ds(pl.multiple_of(d * rows + core * half, half), half)],
-            hs_send.at[k - 1], hs_recv.at[k - 1], {"dp": to},
+            h_ref.at[
+                pl.ds(pl.multiple_of(mine * quarter, quarter), quarter),
+                pl.ds(pl.multiple_of(to * depth, depth), depth),
+            ],
+            piece(d, mine), hs_send.at[k - 1], hs_recv.at[k - 1], {"dp": to},
         )
         copy.start()
         hidden_sends.append(copy)
@@ -89,19 +104,23 @@
 
     project(d * rows, rows, store_own)
 
-    forwards, partial_sends = [], []
-    for k in range(1, nd):
-        s = lax.rem(d + nd - k, nd)
-        for turn in range(2):
-            part = core if turn == 0 else 1 - core
-            block = spread.at[pl.ds(pl.multiple_of(s * rows + part * half, half), half)]
+    forwards, crossings, partial_sends = [], [], []
+    for turn in range(2):
+        for k in range(1, nd):
+            s = flip(d, k)
+            part = side if turn == 0 else 1 - side
+            got = piece(s, 2 * part + core)
+            to_mate = remote(got, got, hf_send.at[k - 1, turn], hf_recv.at[k - 1, turn], {"vocab": mate})
+            over = remote(got, got, hx_send.at[k - 1], hx_recv.at[k - 1], {"vocab": across})
             if turn == 0:
-                remote(block, block, hs_send.at[k - 1], hs_recv.at[k - 1], {"dp": s}).wait_recv()
-                copy = remote(block, block, hf_send.at[k - 1], hf_recv.at[k - 1], {"vocab": mate})
-                copy.start()
-                forwards.append(copy)
+                remote(got, got, hs_send.at[k - 1], hs_recv.at[k - 1], {"dp": s}).wait_recv()
+                over.start()
+                crossings.append(over)
             else:
-                remote(block, block, hf_send.at[k - 1], hf_recv.at[k - 1], {"vocab": mate}).wait_recv()
+                over.wait_recv()
+            to_mate.start()
+            forwards.append(to_mate)
+            to_mate.wait_recv()
             there = pl.ds(pl.multiple_of(part * half, half), half)
 
             def store_part(cols, value):
@@ -136,7 +155,7 @@
         copy.wait_recv()
     for k in range(1, nd):
         for turn in range(2):
-            part = core if turn == 0 else 1 - core
+            part = side if turn == 0 else 1 - side
             there = pl.ds(pl.multiple_of(part * half, half), half)
             ucol[k - 1, there, :] = jnp.broadcast_to(urecv[k - 1, turn][0:1, :], (128, half)).T
 
@@ -191,19 +210,26 @@
         return 0
 
     lax.fori_loop(0, rows // step_rows, differentiate, 0)
+    relayed = nd == 4
     grad_sends = []
-    for k in range(1, nd):
+    for k in range(1, nd - 1 if relayed else nd):
         copy = remote(
             grads.at[own_rows], grads.at[own_rows], g_send.at[k - 1], g_recv.at[k - 1],
-            {"dp": lax.rem(d + k, nd)},
+            {"dp": flip(d, k)},
         )
         copy.start()
         grad_sends.append(copy)
 
+    def relay(k):
+        block = grads.at[pl.ds(pl.multiple_of(flip(d, k) * rows + (k - 1) * half, half), half)]
+        return remote(block, block, x_send.at[k - 1], x_recv.at[k - 1], {"dp": flip(d, 3 - k)})
+
+    relays = [relay(1), relay(2)] if relayed else []
+
     depth_tile = min(256, depth)
 
     def pull(k):
-        s = lax.rem(d + nd - k, nd)
+        s = flip(d, k)
 
         def step(n, _):
             at = pl.ds(pl.multiple_of(n * depth_tile, depth_tile), depth_tile)
@@ -218,7 +244,7 @@
         lax.fori_loop(0, depth // depth_tile, step, 0)
 
     def ahead(b):
-        s = lax.rem(d + nd - b // per, nd)
+        s = flip(d, b // per)
         return s * per + b % per - v + nv
 
     def partner(level):
@@ -262,17 +288,32 @@
         if level + 1 < levels:
             send(b, level + 1)
 
+    def arrive(k):
+        if relayed and k == nd - 1:
+            for copy in relays:
+                copy.wait_recv()
+        elif k:
+            grad_sends[k - 1].wait_recv()
+            if relayed:
+                relays[k - 1].start()
+
+    pending = []
     for k in range(nd):
-        if k:
-            grad_sends[k - 1].wait_recv()
+        if relayed and k == 1:
+            arrive(1)
+            arrive(2)
+        elif not (relayed and k == 2):
+            arrive(k)
         pull(k)
         for j in range(per):
             send(k * per + j, 0)
-        if k:
-            for j in range(per):
-                receive((k - 1) * per + j, 0)
-    for j in range(per):
-        receive((nd - 1) * per + j, 0)
+        for j in range(per):
+            receive(k * per + j, 0)
+            pending.append(k * per + j)
+        if k >= 2 and levels > 1:
+            for b in pending[:per]:
+                receive(b, 1)
+            pending = pending[per:]
 
     def weigh(n, _):
         at = pl.ds(pl.multiple_of(n * depth_tile, depth_tile), depth_tile)
@@ -285,7 +326,7 @@
     lax.fori_loop(0, depth // depth_tile, weigh, 0)
 
     for level in range(1, levels):
-        for b in range(nv):
+        for b in pending if level == 1 else range(nv):
             receive(b, level)
     for b in range(nv):
         @pl.when(ahead(b) == nv)
@@ -299,7 +340,7 @@
         def _(b=b):
             hop(b, 0).wait_send()
 
-    for copy in hidden_sends + forwards + partial_sends + stat_sends + grad_sends:
+    for copy in hidden_sends + forwards + crossings + partial_sends + stat_sends + grad_sends + relays:
         copy.wait_send()
     for n in range(depth // depth_tile):
         at = pl.ds(n * depth_tile, depth_tile)
@@ -345,10 +386,11 @@
             pltpu.VMEM((nd - 1, 2, 8, rows // 2), F32),
             pltpu.VMEM((nd - 1, rows, 128), F32),
             dma, dma, dma((depth // min(256, depth),)),
-            dma((nd - 1,)), dma((nd - 1,)), dma((nd - 1,)), dma((nd - 1,)),
+            dma((nd - 1,)), dma((nd - 1,)), dma((nd - 1, 2)), dma((nd - 1, 2)), dma((nd - 1,)), dma((nd - 1,)),
             dma((nd - 1, 2)), dma((nd - 1, 2)), dma((nd - 1, 2)), dma((nd - 1, 2)),
             dma((nv - 1,)), dma((nv - 1,)),
             dma((nd - 1,)), dma((nd - 1,)),
+            dma((2,)), dma((2,)),
             dma((nv,)), dma((levels, nv)),
         ],
         compiler_params=pltpu.CompilerParams(

time: 146 us -> 127 us (0.87)
  the two profiles are of different devices: /device:TPU:8 before, /device:TPU:6 now
where the time goes in v2:
time: 127 us
  Pallas kernels  119 us (94%)
  local copies, waits for them, and re-layouts  7.75 us (6%)
    pallas_call x1, Pallas kernels, shards(): pl.pallas_call(functools.partial(kernel, nd, nv, levels), out_shape=(jax....  119 us
    unnamed x3, local copies, waits for them, and re-layouts  7.75 us

profile of v2, /device:TPU:6, one launch (start us, length us, event | category | flops | bytes accessed | tf_op | source)
XLA Modules:
  0.0 127.2 jit_solution(12067346289127820892)
XLA Ops:
  0.6 118.8 %token_loss.1 = (f32[1,256]{1,0:T(1,128)}, bf16[128,2048]{1,0:T(8,128)(2,1)}, bf16[2048,1024]{1,0:T(8,128)(2,1)}) custom-call(bf16[256,8192]{1,0:T(8,128)(2,1)} %h_ref.1, bf16[2048,1024]{1,0:T(8,128)(2,1)} %w_hbm.1, s32[1,256]{1,0:T(1,128)} %bitcast.4, f32[1,256]{1,0:T(1,128)} %bitcast.5), custom_call_target="tpu_custom_call" | custom-call | flops 12884901888 | bytes 16777216 | tf_op jit(solution)/shard_map/token_loss/pallas_call | solution.py:360
  119.4 1.2 copy.10
  120.6 1.9 %copy.11 = bf16[128,2048]{1,0:T(8,128)(2,1)} copy(bf16[128,2048]{1,0:T(8,128)(2,1)} %get-tuple-element.13) | data formatting | bytes 1048576
  122.5 4.6 %copy.12 = bf16[2048,1024]{1,0:T(8,128)(2,1)} copy(bf16[2048,1024]{1,0:T(8,128)(2,1)} %get-tuple-element.14) | data formatting | bytes 8388608
